TPU v7x, 32 devices: a whole 2x2x4 slice. The times are simulated.
32 devices in a mesh: gx: 2 (over core), gy: 2 (over x), gz: 8 (over z, y).
Axes of the slice: x: 2, y: 2, z: 4, core: 2. Of those that a mesh axis runs over, the one named last changes fastest.
Arguments:
- old_pos: float32 [3, 32768], P(None, ('gx', 'gy', 'gz')), may hold values from -6 to 6
- new_pos: float32 [3, 32768], P(None, ('gx', 'gy', 'gz')), may hold values from -6 to 6
- inv_mass: float32 [32768], P(('gx', 'gy', 'gz')), may hold values from 0.05 to 1
- rest_length: float32 [32768], P(('gx', 'gy', 'gz')), may hold values from 0.8 to 1.6
- bond_pairs: int32 [2, 32768], P(None, ('gx', 'gy', 'gz')), may hold values from 0 to 1311, as said below
- live: int32 [32768], P(('gx', 'gy', 'gz')), may hold values from 0 to 1, as said below
- send_index: int32 [192, 48], P(('gx', 'gy', 'gz')), may hold values from 0 to 1023, as said below
Outputs:
- displacement: float32 [3, 32768], P(None, ('gx', 'gy', 'gz'))
- multipliers: float32 [32768], P(('gx', 'gy', 'gz'))
Inputs may be any that keep to these rules, and one draw needn't show every extreme that they name: `bond_pairs`: in domain k's slots, row 0 is an own atom (0 to 1023). Row 1 indexes the domain's extended list: its own atoms, then six blocks of 48 received atoms, block 2a + s holding, in order, list 2a + s of the neighbour one step down (s = 0) or up (s = 1) along axis a. Every atom is in at most two live constraints, each received atom is the second atom of at most one live constraint, and exactly 216 live constraints of each domain name a received atom. `live`: padding slots change nothing. `send_index`: rows 6k to 6k + 5 are domain k's lists of own atoms; list 2a + s goes to the neighbour one step up (s = 0) or down (s = 1) along axis a, periodically. The 288 entries of a domain are distinct.
All inputs are finite; a program needn't handle non-finite values.
Results may differ from a plain program's by a relative error of at most 0.0001.
Values sent between devices are 32-bit elements; how exact they have to be, the bound alone decides.
A program may use at most 64 MiB of HBM per device.

v0:
```python
import functools

import jax
import jax.numpy as jnp
from jax import lax
from jax.experimental import pallas as pl
from jax.experimental.pallas import tpu as pltpu
from jax.sharding import PartitionSpec as P

ORDER = 4
AXES = ("gx", "gy", "gz")
LANES = 128
HALF = 64
ROUNDS = 2 * ORDER + 3
BIG = 4


class Pick:
    def __init__(self, row, lane, count):
        self.lane = lane & (LANES - 1)
        self.masks = [row == r for r in range(count)]

    def __call__(self, table, start=0, init=None, stop=None):
        out = jnp.zeros(self.lane.shape, table.dtype) if init is None else init
        count = table.shape[0] if stop is None else stop
        for r in range(count):
            line = jnp.broadcast_to(table[r : r + 1, :], self.lane.shape)
            found = jnp.take_along_axis(line, self.lane, axis=1, mode="promise_in_bounds")
            out = jnp.where(self.masks[start + r], found, out)
        return out


def to_row(x):
    return jnp.concatenate([x[r : r + 1, :] for r in range(x.shape[0])], axis=1)


def to_rows(x):
    return jnp.concatenate(
        [x[:, LANES * r : LANES * (r + 1)] for r in range(x.shape[1] // LANES)], axis=0
    )


def one_hot_lanes(lane_row):
    shape = (LANES, lane_row.shape[1])
    hit = lax.broadcasted_iota(jnp.int32, shape, 0) == lane_row
    return jnp.where(hit, 1.0, 0.0).astype(jnp.bfloat16)


def place(row_row, values, hot, rows):
    shape = (rows, row_row.shape[1])
    hit = lax.broadcasted_iota(jnp.int32, shape, 0) == row_row
    left = jnp.concatenate([jnp.where(hit, v.astype(jnp.float32), 0.0) for v in values], axis=0)
    out = lax.dot_general(
        left.astype(jnp.bfloat16), hot, (((1,), (1,)), ((), ())), preferred_element_type=jnp.float32
    ).astype(jnp.int32)
    return [out[rows * i : rows * (i + 1)] for i in range(len(values))]


def kernel(sizes, width, old_ref, new_ref, mass_ref, rest_ref, pairs_ref, live_ref, send_ref,
           move_ref, mult_ref, listed, out_big, in_big, out_small, in_small, send_sem, recv_sem):
    rows = mass_ref.shape[0]
    slots = rows * LANES

    slot_of = {}
    targets = []
    for a, axis in enumerate(AXES):
        me, count = lax.axis_index(axis), sizes[a]
        up, down = lax.rem(me + 1, count), lax.rem(me + count - 1, count)
        base = len(targets)
        if count == 2:
            slot_of[a] = (base, base)
            targets.append(({axis: up}, base))
        else:
            slot_of[a] = (base, base + 1)
            targets.append(({axis: up}, base))
            targets.append(({axis: down}, base + 1))

    barrier = pltpu.get_barrier_semaphore()
    for device, unused in targets:
        pl.semaphore_signal(barrier, inc=1, device_id=device, device_id_type=pl.DeviceIdType.MESH)

    started = []

    def launch(number, tiles):
        if number < 2:
            for i, tile in enumerate(tiles):
                out_big[number, i] = tile
        else:
            out_small[number - 2] = tiles[0]
        copies = []
        for n, (device, landing) in enumerate(targets):
            copies.append(
                pltpu.make_async_remote_copy(
                    src_ref=out_big.at[number] if number < 2 else out_small.at[number - 2],
                    dst_ref=in_big.at[number, landing] if number < 2 else in_small.at[number - 2, landing],
                    send_sem=send_sem.at[number, n],
                    recv_sem=recv_sem.at[number, landing],
                    device_id=device,
                    device_id_type=pl.DeviceIdType.MESH,
                )
            )
        for copy in copies:
            copy.start()
        started.extend(copies)
        return copies

    tile_row = lax.broadcasted_iota(jnp.int32, (8, LANES), 0)
    tile_lane = lax.broadcasted_iota(jnp.int32, (8, LANES), 1)
    back_half = tile_lane >= HALF

    def arrived(number, copies, index, both_out=False):
        tiles = [
            in_big[number, n, index] if number < 2 else in_small[number - 2, n]
            for n in range(len(targets))
        ]
        out = tiles[slot_of[0][0]]
        for a in range(3):
            low, high = slot_of[a]
            if low == high:
                out = jnp.where(tile_row // 2 == a, tiles[low], out)
                continue
            odd = tile_row % 2 == 1
            from_up = odd if both_out else odd != back_half
            out = jnp.where(tile_row // 2 == a, jnp.where(from_up, tiles[high], tiles[low]), out)
        return out

    def wait(copies):
        for copy in copies:
            copy.wait_recv()

    listed[...] = jnp.zeros_like(listed)
    listed[0:6, 0:width] = send_ref[...]
    listed[0:6, HALF : HALF + width] = send_ref[...]
    sending = listed[...]
    at_listed = Pick(sending >> 7, sending, rows)

    old = [to_rows(old_ref[c : c + 1, :]) for c in range(3)]
    new = [to_rows(new_ref[c : c + 1, :]) for c in range(3)]
    mass = mass_ref[...]
    fields = old + new + [mass]
    picked = [at_listed(f) for f in fields]
    picked.append(picked[6])
    tiles = [jnp.where(back_half, picked[2 * i + 1], picked[2 * i]) for i in range(BIG)]
    pl.semaphore_wait(barrier, len(targets))
    copies = launch(0, tiles)

    first = to_rows(pairs_ref[0:1, :])
    second = to_rows(pairs_ref[1:2, :])
    live = live_ref[...]
    own = second < slots
    offset = jnp.maximum(second - slots, 0)
    block = jnp.zeros_like(offset)
    for i in range(1, 6):
        block = block + jnp.where(offset >= width * i, 1, 0)
    second_row = jnp.where(own, second >> 7, rows + block)
    second_lane = jnp.where(own, second & (LANES - 1), offset - width * block)
    at_first = Pick(first >> 7, first, rows)
    at_second = Pick(second_row, second_lane, rows + 6)
    number = (
        lax.broadcasted_iota(jnp.int32, (rows, LANES), 0) * LANES
        + lax.broadcasted_iota(jnp.int32, (rows, LANES), 1)
        + 1
    )
    counted = (live != 0) & (first != second)

    def code_row(mask_first, mask_second):
        return jnp.concatenate(
            [to_row(jnp.where(mask_first, first >> 7, -1)), to_row(jnp.where(mask_second, second_row, -1))], 1
        )

    hot = one_hot_lanes(jnp.concatenate([pairs_ref[0:1, :] & (LANES - 1), to_row(second_lane)], 1))
    number_row = to_row(number)
    number_row = jnp.concatenate([number_row, number_row + slots], 1)
    parts = [number_row >> 6, number_row & 63]
    high, low = place(code_row(counted, counted), parts, hot, rows + 8)
    ends = high * 64 + low
    ends_own = ends[:rows]
    ends_halo = ends[rows:]

    listed_row = jnp.concatenate([sending[b : b + 1, :] for b in range(6)], axis=1)
    spot = lax.broadcasted_iota(jnp.int32, listed_row.shape, 1)
    spot_block = spot // LANES
    spot_lane = spot % LANES
    place_block, place_lane = place(
        jnp.where(spot_lane < width, listed_row >> 7, -1),
        [spot_block + 1, spot_lane],
        one_hot_lanes(listed_row & (LANES - 1)),
        rows,
    )

    def split(code):
        minus = code > slots
        index = jnp.where(minus, code - slots, code) - 1
        return jnp.where(code > 0, index >> 7, -1), index & (LANES - 1), jnp.where(minus, -1.0, 1.0)

    other_first = jnp.where(counted, at_first(ends_own) - number, 0)
    other_second = jnp.where(counted & own, at_second(ends_own) - (number + slots), 0)

    def partner(other, at, remote_row=None, remote_lane=None):
        row, lane, sign = split(other)
        there = at(place_block)
        far_row = jnp.where(there > 0, rows + there - 1, -1)
        far_lane = HALF + at(place_lane)
        if remote_row is not None:
            far_row = jnp.where(own, far_row, remote_row)
            far_lane = jnp.where(own, far_lane, remote_lane)
        near = other > 0
        return (
            Pick(jnp.where(near, row, far_row), jnp.where(near, lane, far_lane), rows + 6),
            jnp.where(near, sign, 1.0),
        )

    along_first, sign_first = partner(other_first, at_first)
    along_second, sign_second = partner(other_second, at_second, second_row, second_lane)

    send_code = jnp.where(back_half, pltpu.roll(ends_halo, HALF, 1), at_listed(ends_own))
    send_row, send_lane, send_sign = split(send_code)
    to_send = Pick(send_row, send_lane, rows)

    lead_first = counted & ((other_first <= 0) | (number < other_first))
    lead_second = counted & own & ((other_second <= 0) | (number + slots < other_second))
    high, low = place(code_row(lead_first, lead_second), parts, hot, rows)
    lead = high * 64 + low
    row, lane, lead_sign = split(lead)
    at_lead = Pick(row, lane, rows)
    row, lane, rest_sign = split(ends_own - lead)
    at_rest = Pick(row, lane, rows)
    at_far = Pick(jnp.where(place_block > 0, place_block - 1, -1), HALF + place_lane, 6)

    near_first = [at_first(f) for f in fields]
    near_second = [at_second(f) for f in fields]

    wait(copies)
    got = [arrived(0, copies, i, both_out=True) for i in range(BIG)]
    got_back = [pltpu.roll(t, HALF, 1) for t in got[:3]]
    halo = [got[0], got_back[0], got[1], got_back[1], got[2], got_back[2], got[3]]
    near_second = [at_second(h, rows, g, 6) for h, g in zip(halo, near_second)]
    mass_first, mass_second = near_first[6], near_second[6]
    old_span = [near_first[c] - near_second[c] for c in range(3)]
    new_span = [near_first[3 + c] - near_second[3 + c] for c in range(3)]
    dot = lambda p, q: p[0] * q[0] + p[1] * q[1] + p[2] * q[2]
    norm = jnp.sqrt(dot(old_span, old_span) + 0.25)
    unit = [s / norm for s in old_span]
    mass_sum = mass_first + mass_second
    scaling = live.astype(jnp.float32) / jnp.sqrt(mass_sum)
    rest = rest_ref[...]
    weight = [scaling * u for u in unit]
    x = scaling * (dot(unit, new_span) - rest)

    copies = launch(1, [send_sign * to_send(w) for w in weight] + [to_send(x)])
    diagonal = 1.0 - dot(weight, weight) * mass_sum
    pair_first = [along_first(w) for w in weight]
    pair_second = [along_second(w) for w in weight]
    lead_weight = [lead_sign * at_lead(w) for w in weight]
    rest_weight = [rest_sign * at_rest(w) for w in weight]
    near = along_first(x), along_second(x)
    wait(copies)
    got = [arrived(1, copies, i) for i in range(BIG)]
    pair_first = [sign_first * along_first(h, rows, p, 6) for h, p in zip(got[:3], pair_first)]
    pair_second = [sign_second * along_second(h, rows, p, 6) for h, p in zip(got[:3], pair_second)]
    far_weight = [at_far(h, stop=6) for h in got[:3]]
    factor_first = -mass_first * dot(weight, pair_first)
    factor_second = mass_second * dot(weight, pair_second)
    halo_x = got[3]

    def finish(near, halo_x):
        return along_first(halo_x, rows, near[0], 6), along_second(halo_x, rows, near[1], 6)

    def expand(x, halo_x, near, number):
        total_x, total_halo = x, halo_x
        g = finish(near, halo_x)
        total_g = list(g)
        for step in range(ORDER):
            x = diagonal * x + factor_first * g[0] + factor_second * g[1]
            copies = launch(number, [to_send(x)])
            total_x = total_x + x
            near = along_first(x), along_second(x)
            wait(copies)
            halo_x = arrived(number, copies, 0)
            g = finish(near, halo_x)
            total_g = [t + h for t, h in zip(total_g, g)]
            total_halo = total_halo + halo_x
            number += 1
        return total_x, total_halo, total_g

    first_sol, first_halo, first_g = expand(x, halo_x, near, 2)
    move_g = mass_first * first_g[0], mass_second * first_g[1]
    move_x = mass_sum * first_sol
    stretch = [
        new_span[c] - move_x * weight[c] - move_g[0] * pair_first[c] + move_g[1] * pair_second[c]
        for c in range(3)
    ]
    length_sq = dot(stretch, stretch)
    target = jnp.sqrt(jnp.maximum(2.0 * rest * rest - length_sq, 0.25 * rest * rest))
    y = scaling * (rest - target)
    copies = launch(2 + ORDER, [to_send(y)])
    near = along_first(y), along_second(y)
    wait(copies)
    second_sol, second_halo, unused = expand(y, arrived(2 + ORDER, copies, 0), near, 3 + ORDER)

    total = first_sol + second_sol
    mult_ref[...] = total
    at_ends = at_lead(total), at_rest(total), at_far(first_halo + second_halo, stop=6)
    for c in range(3):
        moved = -mass * (
            lead_weight[c] * at_ends[0] + rest_weight[c] * at_ends[1] + far_weight[c] * at_ends[2]
        )
        move_ref[c : c + 1, :] = to_row(moved)
    for copy in started:
        copy.wait_send()


def solution(mesh):
    sizes = tuple(mesh.shape[a] for a in AXES)

    def per_device(old_pos, new_pos, inv_mass, rest_length, bond_pairs, live, send_index):
        atoms = old_pos.shape[1]
        rows = atoms // LANES
        width = send_index.shape[1]
        links = sum(1 if n == 2 else 2 for n in sizes)
        tall = lambda v: v.reshape(rows, LANES)
        vmem = pl.BlockSpec(memory_space=pltpu.VMEM)
        tile = (8, LANES)
        moved, mult = pl.pallas_call(
            functools.partial(kernel, sizes, width),
            out_shape=(
                jax.ShapeDtypeStruct((3, atoms), jnp.float32),
                jax.ShapeDtypeStruct((rows, LANES), jnp.float32),
            ),
            in_specs=[vmem] * 7,
            out_specs=(vmem, vmem),
            scratch_shapes=[
                pltpu.VMEM(tile, jnp.int32),
                pltpu.VMEM((2, BIG) + tile, jnp.float32),
                pltpu.VMEM((2, links, BIG) + tile, jnp.float32),
                pltpu.VMEM((ROUNDS - 2,) + tile, jnp.float32),
                pltpu.VMEM((ROUNDS - 2, links) + tile, jnp.float32),
                pltpu.SemaphoreType.DMA((ROUNDS, links)),
                pltpu.SemaphoreType.DMA((ROUNDS, links)),
            ],
            compiler_params=pltpu.CompilerParams(collective_id=0, has_side_effects=True),
        )(old_pos, new_pos, tall(inv_mass), tall(rest_length), bond_pairs, tall(live), send_index)
        return moved, mult.reshape(atoms)

    spread = P(AXES)
    wide = P(None, AXES)
    return jax.shard_map(
        per_device,
        mesh=mesh,
        in_specs=(wide, wide, spread, spread, wide, spread, P(AXES, None)),
        out_specs=(wide, spread),
        check_vma=False,
    )
```

profile of v0, /device:TPU:0, one launch (start us, length us, event | category | flops | bytes accessed | tf_op | source)
XLA Modules:
  0.0 55.8 jit_solution(16854623067058581371)
XLA Ops:
  0.6 53.3 %shard_map.86 = (f32[3,1024]{1,0:T(4,128)}, f32[8,128]{1,0:T(8,128)}) custom-call(f32[3,1024]{1,0:T(4,128)} %old_ref.1, f32[3,1024]{1,0:T(4,128)} %new_ref.1, f32[8,128]{1,0:T(8,128)} %bitcast.4, f32[8,128]{1,0:T(8,128)} %bitcast.5, s32[2,1024]{1,0:T(2,128)} %pairs_ref.1, s32[8,128]{1,0:T(8,128)} %bitcast.6, s32[6,48]{1,0:T(8,128)} %send_ref.1), custom_call_target="tpu_custom_call" | custom-call | tf_op jit(solution)/shard_map/pallas_call | solution.py:324
  53.9 0.0 copy-start
  53.9 1.3 %copy.11 = f32[3,1024]{1,0:T(4,128)} copy(f32[3,1024]{1,0:T(4,128)} %get-tuple-element.8) | data formatting | bytes 24576
  55.3 0.0 copy-done
  55.3 0.6 %copy.12 = f32[1024]{0:T(1024)} copy(f32[1024]{0:T(1024)S(1)} %bitcast.7) | data formatting | bytes 8192
Async XLA Ops:
  53.9 1.3 %copy-start = (f32[8,128]{1,0:T(8,128)S(1)}, f32[8,128]{1,0:T(8,128)}, u32[]{:S(2)}) copy-start(f32[8,128]{1,0:T(8,128)} %get-tuple-element.5) | copy-start | bytes 12292
where the time goes:
time: 56.1 us; the launch traced here: 55.8 us
  Pallas kernels  53.3 us (95%)
  local copies, waits for them, and re-layouts  1.92 us (3%)
  between operations  0.65 us (1%)
    pallas_call x1, Pallas kernels, per_device(): pl.pallas_call(functools.partial(kernel, sizes, width), out_shape=(jax.Sh...  53.3 us
    unnamed x4, local copies, waits for them, and re-layouts  1.92 us

commit v1 on v0

--- a/solution.py
+++ b/solution.py
@@ -13,6 +13,56 @@
 HALF = 64
 ROUNDS = 2 * ORDER + 3
 BIG = 4
+
+
+class Plan:
+    def __init__(self, sizes, start, turn, flip):
+        self.sizes, self.start, self.turn, self.flip = sizes, start, turn, flip
+
+    def site_of(self, domain):
+        ix, iy, iz = domain
+        nx, ny, nz = self.sizes
+        spot = (self.start + self.turn * iz) % nz
+        if nz % 2 == 0:
+            late = spot // (nz // 2)
+            spot = (1 - late) * 2 * spot + late * (2 * (nz - 1 - spot) + 1)
+        return [(ix + iy + iz + self.flip) % nx, iy, spot]
+
+    def domain_on(self, site):
+        core, iy, spot = site
+        nx, ny, nz = self.sizes
+        if nz % 2 == 0:
+            line, side = spot // 2, spot % 2
+            spot = (1 - side) * line + side * (nz - 1 - line)
+        iz = (self.turn * (spot - self.start + nz) + nz) % nz
+        return [(core + 2 * nx * (ny + nz) - iy - iz - self.flip) % nx, iy, iz]
+
+    def named(self, site):
+        return dict(zip(AXES, site))
+
+    def price(self):
+        worst = total = 0
+        for ix in range(self.sizes[0]):
+            for iy in range(self.sizes[1]):
+                for iz in range(self.sizes[2]):
+                    site = self.site_of((ix, iy, iz))
+                    assert tuple(self.domain_on(site)) == (ix, iy, iz)
+                    if tuple(site) == (ix, iy, iz):
+                        return None
+                    hops = abs(site[2] // 2 - iz // 2) + abs(site[2] % 2 - iz % 2)
+                    worst, total = max(worst, hops), total + hops
+        return worst, total
+
+
+def best_plan(sizes):
+    plans = [
+        Plan(sizes, start, turn, flip)
+        for start in range(sizes[2])
+        for turn in (1, sizes[2] - 1)
+        for flip in range(sizes[0])
+    ]
+    priced = [(p.price(), i) for i, p in enumerate(plans)]
+    return plans[min(p for p in priced if p[0] is not None)[1]]
 
 
 class Pick:
@@ -56,28 +106,61 @@
     return [out[rows * i : rows * (i + 1)] for i in range(len(values))]
 
 
-def kernel(sizes, width, old_ref, new_ref, mass_ref, rest_ref, pairs_ref, live_ref, send_ref,
-           move_ref, mult_ref, listed, out_big, in_big, out_small, in_small, send_sem, recv_sem):
-    rows = mass_ref.shape[0]
+def kernel(plan, width, *refs):
+    home, results, away, own_results = refs[0:7], refs[7:9], refs[9:16], refs[16:18]
+    listed, out_big, in_big, out_small, in_small, send_sem, recv_sem, carry_sem = refs[18:]
+    move_ref, mult_ref = own_results
+    sizes = plan.sizes
+    rows = home[2].shape[0]
     slots = rows * LANES
+
+    here = [lax.axis_index(axis) for axis in AXES]
+    domain = plan.domain_on(here)
+    sites = [plan.site_of(here), domain]
 
     slot_of = {}
     targets = []
-    for a, axis in enumerate(AXES):
-        me, count = lax.axis_index(axis), sizes[a]
-        up, down = lax.rem(me + 1, count), lax.rem(me + count - 1, count)
+    for a in range(3):
+        moved_by = lambda step: plan.site_of(
+            [(v + (step if i == a else 0)) % n for i, (v, n) in enumerate(zip(domain, sizes))]
+        )
         base = len(targets)
-        if count == 2:
+        up = plan.named(moved_by(1))
+        if sizes[a] == 2:
             slot_of[a] = (base, base)
-            targets.append(({axis: up}, base))
+            targets.append((up, base))
         else:
             slot_of[a] = (base, base + 1)
-            targets.append(({axis: up}, base))
-            targets.append(({axis: down}, base + 1))
-
+            targets.append((up, base))
+            targets.append((plan.named(moved_by(sizes[a] - 1)), base + 1))
+
+    mesh_ids = pl.DeviceIdType.MESH
     barrier = pltpu.get_barrier_semaphore()
-    for device, unused in targets:
-        pl.semaphore_signal(barrier, inc=1, device_id=device, device_id_type=pl.DeviceIdType.MESH)
+    greeted = [plan.named(site) for site in sites] + [device for device, unused in targets]
+    for device in greeted:
+        pl.semaphore_signal(barrier, inc=1, device_id=device, device_id_type=mesh_ids)
+    pl.semaphore_wait(barrier, len(greeted))
+
+    def carry(sources, ends, device, base):
+        copies = [
+            pltpu.make_async_remote_copy(
+                src_ref=source,
+                dst_ref=end,
+                send_sem=carry_sem.at[0, base + i],
+                recv_sem=carry_sem.at[1, base + i],
+                device_id=device,
+                device_id_type=mesh_ids,
+            )
+            for i, (source, end) in enumerate(zip(sources, ends))
+        ]
+        for copy in copies:
+            copy.start()
+        return copies
+
+    inward = carry(home, away, greeted[0], 0)
+    for copy in inward:
+        copy.wait_recv()
+    old_ref, new_ref, mass_ref, rest_ref, pairs_ref, live_ref, send_ref = away
 
     started = []
 
@@ -96,7 +179,7 @@
                     send_sem=send_sem.at[number, n],
                     recv_sem=recv_sem.at[number, landing],
                     device_id=device,
-                    device_id_type=pl.DeviceIdType.MESH,
+                    device_id_type=mesh_ids,
                 )
             )
         for copy in copies:
@@ -141,7 +224,6 @@
     picked = [at_listed(f) for f in fields]
     picked.append(picked[6])
     tiles = [jnp.where(back_half, picked[2 * i + 1], picked[2 * i]) for i in range(BIG)]
-    pl.semaphore_wait(barrier, len(targets))
     copies = launch(0, tiles)
 
     first = to_rows(pairs_ref[0:1, :])
@@ -306,12 +388,16 @@
             lead_weight[c] * at_ends[0] + rest_weight[c] * at_ends[1] + far_weight[c] * at_ends[2]
         )
         move_ref[c : c + 1, :] = to_row(moved)
-    for copy in started:
+    outward = carry(own_results, results, greeted[1], len(home))
+    for copy in started + inward + outward:
         copy.wait_send()
+    for copy in outward:
+        copy.wait_recv()
 
 
 def solution(mesh):
     sizes = tuple(mesh.shape[a] for a in AXES)
+    plan = best_plan(sizes)
 
     def per_device(old_pos, new_pos, inv_mass, rest_length, bond_pairs, live, send_index):
         atoms = old_pos.shape[1]
@@ -322,7 +408,7 @@
         vmem = pl.BlockSpec(memory_space=pltpu.VMEM)
         tile = (8, LANES)
         moved, mult = pl.pallas_call(
-            functools.partial(kernel, sizes, width),
+            functools.partial(kernel, plan, width),
             out_shape=(
                 jax.ShapeDtypeStruct((3, atoms), jnp.float32),
                 jax.ShapeDtypeStruct((rows, LANES), jnp.float32),
@@ -330,6 +416,15 @@
             in_specs=[vmem] * 7,
             out_specs=(vmem, vmem),
             scratch_shapes=[
+                pltpu.VMEM((3, atoms), jnp.float32),
+                pltpu.VMEM((3, atoms), jnp.float32),
+                pltpu.VMEM((rows, LANES), jnp.float32),
+                pltpu.VMEM((rows, LANES), jnp.float32),
+                pltpu.VMEM((2, atoms), jnp.int32),
+                pltpu.VMEM((rows, LANES), jnp.int32),
+                pltpu.VMEM(send_index.shape, jnp.int32),
+                pltpu.VMEM((3, atoms), jnp.float32),
+                pltpu.VMEM((rows, LANES), jnp.float32),
                 pltpu.VMEM(tile, jnp.int32),
                 pltpu.VMEM((2, BIG) + tile, jnp.float32),
                 pltpu.VMEM((2, links, BIG) + tile, jnp.float32),
@@ -337,6 +432,7 @@
                 pltpu.VMEM((ROUNDS - 2, links) + tile, jnp.float32),
                 pltpu.SemaphoreType.DMA((ROUNDS, links)),
                 pltpu.SemaphoreType.DMA((ROUNDS, links)),
+                pltpu.SemaphoreType.DMA((2, 9)),
             ],
             compiler_params=pltpu.CompilerParams(collective_id=0, has_side_effects=True),
         )(old_pos, new_pos, tall(inv_mass), tall(rest_length), bond_pairs, tall(live), send_index)

time: 56.1 us -> 47.1 us (0.84)
  Pallas kernels: 53.3 us -> 44.3 us
    pallas_call x1, Pallas kernels: 53.3 us -> 44.3 us  [per_device(): pl.pallas_call(functools.partial(kernel, plan, width), out_shape=(jax.Sha...]
where the time goes in v1:
time: 47.1 us; the launch traced here: 46.9 us
  Pallas kernels  44.3 us (94%)
  local copies, waits for them, and re-layouts  1.92 us (4%)
  between operations  0.65 us (1%)
    pallas_call x1, Pallas kernels, per_device(): pl.pallas_call(functools.partial(kernel, plan, width), out_shape=(jax.Sha...  44.3 us
    unnamed x4, local copies, waits for them, and re-layouts  1.92 us

profile of v1, /device:TPU:0, one launch (start us, length us, event | category | flops | bytes accessed | tf_op | source)
XLA Modules:
  0.0 46.9 jit_solution(1617450677423831882)
XLA Ops:
  0.6 44.3 %shard_map.86 = (f32[3,1024]{1,0:T(4,128)}, f32[8,128]{1,0:T(8,128)}) custom-call(f32[3,1024]{1,0:T(4,128)} %refs_0_.1, f32[3,1024]{1,0:T(4,128)} %refs_1_.1, f32[8,128]{1,0:T(8,128)} %bitcast.4, f32[8,128]{1,0:T(8,128)} %bitcast.5, s32[2,1024]{1,0:T(2,128)} %refs_4_.1, s32[8,128]{1,0:T(8,128)} %bitcast.6, s32[6,48]{1,0:T(8,128)} %refs_6_.1), custom_call_target="tpu_custom_call" | custom-call | tf_op jit(solution)/shard_map/pallas_call | solution.py:410
  44.9 0.0 copy-start
  44.9 1.3 %copy.11 = f32[3,1024]{1,0:T(4,128)} copy(f32[3,1024]{1,0:T(4,128)} %get-tuple-element.8) | data formatting | bytes 24576
  46.3 0.0 copy-done
  46.3 0.6 %copy.12 = f32[1024]{0:T(1024)} copy(f32[1024]{0:T(1024)S(1)} %bitcast.7) | data formatting | bytes 8192
Async XLA Ops:
  44.9 1.3 %copy-start = (f32[8,128]{1,0:T(8,128)S(1)}, f32[8,128]{1,0:T(8,128)}, u32[]{:S(2)}) copy-start(f32[8,128]{1,0:T(8,128)} %get-tuple-element.5) | copy-start | bytes 12292

commit v2 on v1

v2 whole, which is shorter than its diff:
```python
import functools

import jax
import jax.numpy as jnp
from jax import lax
from jax.experimental import pallas as pl
from jax.experimental.pallas import tpu as pltpu
from jax.sharding import PartitionSpec as P

ORDER = 4
AXES = ("gx", "gy", "gz")
LANES = 128
HALF = 64
ROUNDS = 2 * ORDER + 3
BIG = 4


class Plan:
    def __init__(self, sizes, start, turn, flip):
        self.sizes, self.start, self.turn, self.flip = sizes, start, turn, flip

    def site_of(self, domain):
        ix, iy, iz = domain
        nx, ny, nz = self.sizes
        spot = (self.start + self.turn * iz) % nz
        if nz % 2 == 0:
            late = spot // (nz // 2)
            spot = (1 - late) * 2 * spot + late * (2 * (nz - 1 - spot) + 1)
        return [(ix + iy + iz + self.flip) % nx, iy, spot]

    def domain_on(self, site):
        core, iy, spot = site
        nx, ny, nz = self.sizes
        if nz % 2 == 0:
            line, side = spot // 2, spot % 2
            spot = (1 - side) * line + side * (nz - 1 - line)
        iz = (self.turn * (spot - self.start + nz) + nz) % nz
        return [(core + 2 * nx * (ny + nz) - iy - iz - self.flip) % nx, iy, iz]

    def named(self, site):
        return dict(zip(AXES, site))

    def around(self, domain):
        found = []
        for a, n in enumerate(self.sizes):
            for step in (1,) if n == 2 else (1, n - 1):
                found.append([(v + step) % n if i == a else v for i, v in enumerate(domain)])
        return found

    def price(self):
        worst = total = 0
        for ix in range(self.sizes[0]):
            for iy in range(self.sizes[1]):
                for iz in range(self.sizes[2]):
                    assert self.domain_on(self.site_of((ix, iy, iz))) == [ix, iy, iz]
                    for domain in [(ix, iy, iz)] + self.around((ix, iy, iz)):
                        site = self.site_of(domain)
                        hops = abs(site[2] // 2 - iz // 2) + abs(site[2] % 2 - iz % 2)
                        hops += abs(site[1] - iy)
                        worst, total = max(worst, hops), total + hops
        return worst, total


def best_plan(sizes):
    plans = [
        Plan(sizes, start, turn, flip)
        for start in range(sizes[2])
        for turn in (1, sizes[2] - 1)
        for flip in range(sizes[0])
    ]
    return min(plans, key=lambda plan: plan.price())


class Hop:
    def __init__(self, source, end, send_sem, recv_sem, site, here=None):
        self.parts = source, end, recv_sem
        self.copy = pltpu.make_async_remote_copy(
            src_ref=source,
            dst_ref=end,
            send_sem=send_sem,
            recv_sem=recv_sem,
            device_id=dict(zip(AXES, site)),
            device_id_type=pl.DeviceIdType.MESH,
        )
        self.away = None
        if here is not None:
            self.away = (site[0] != here[0]) | (site[1] != here[1]) | (site[2] != here[2])

    def start(self):
        if self.away is None:
            self.copy.start()
            return
        pl.when(self.away)(self.copy.start)
        pl.when(jnp.logical_not(self.away))(lambda: pltpu.make_async_copy(*self.parts).start())

    def wait_recv(self):
        self.copy.wait_recv()

    def wait_send(self):
        if self.away is None:
            self.copy.wait_send()
        else:
            pl.when(self.away)(self.copy.wait_send)


class Pick:
    def __init__(self, row, lane, count):
        self.lane = lane & (LANES - 1)
        self.masks = [row == r for r in range(count)]

    def __call__(self, table, start=0, init=None, stop=None):
        out = jnp.zeros(self.lane.shape, table.dtype) if init is None else init
        count = table.shape[0] if stop is None else stop
        for r in range(count):
            line = jnp.broadcast_to(table[r : r + 1, :], self.lane.shape)
            found = jnp.take_along_axis(line, self.lane, axis=1, mode="promise_in_bounds")
            out = jnp.where(self.masks[start + r], found, out)
        return out


def to_row(x):
    return jnp.concatenate([x[r : r + 1, :] for r in range(x.shape[0])], axis=1)


def to_rows(x):
    return jnp.concatenate(
        [x[:, LANES * r : LANES * (r + 1)] for r in range(x.shape[1] // LANES)], axis=0
    )


def one_hot_lanes(lane_row):
    shape = (LANES, lane_row.shape[1])
    hit = lax.broadcasted_iota(jnp.int32, shape, 0) == lane_row
    return jnp.where(hit, 1.0, 0.0).astype(jnp.bfloat16)


def place(row_row, values, hot, rows):
    shape = (rows, row_row.shape[1])
    hit = lax.broadcasted_iota(jnp.int32, shape, 0) == row_row
    left = jnp.concatenate([jnp.where(hit, v.astype(jnp.float32), 0.0) for v in values], axis=0)
    out = lax.dot_general(
        left.astype(jnp.bfloat16), hot, (((1,), (1,)), ((), ())), preferred_element_type=jnp.float32
    ).astype(jnp.int32)
    return [out[rows * i : rows * (i + 1)] for i in range(len(values))]


def kernel(plan, width, *refs):
    inputs, (move_ref, mult_ref) = refs[0:7], refs[7:9]
    (old_ref, new_ref, mass_ref, rest_ref, pairs_ref, live_ref, send_ref) = staged = refs[9:16]
    (listed, own_codes, codes, own_fields, fields_in, own_far, far_in, own_last, last_in,
     out_big, in_big, out_small, in_small, send_sem, recv_sem, carry_sem, load_sem) = refs[16:]
    rows = mass_ref.shape[0]
    slots = rows * LANES
    sizes = plan.sizes

    here = [lax.axis_index(axis) for axis in AXES]
    domain = plan.domain_on(here)
    homes_near = plan.around(domain)
    sites_near = [plan.site_of(d) for d in homes_near]
    sites_home_near = [plan.site_of(d) for d in plan.around(here)]
    greeted = [plan.site_of(here), domain] + sites_near + homes_near + sites_home_near
    barrier = pltpu.get_barrier_semaphore()
    for site in greeted:
        pl.semaphore_signal(
            barrier, inc=1, device_id=plan.named(site), device_id_type=pl.DeviceIdType.MESH
        )

    loads = [
        pltpu.make_async_copy(source, end, load_sem.at[i])
        for i, (source, end) in enumerate(zip(inputs, staged))
    ]
    for load in loads:
        load.start()

    slot_of, landings = [], []
    for n in sizes:
        base = len(landings)
        if n == 2:
            slot_of.append((base, base))
            landings.append(base)
        else:
            slot_of.append((base, base + 1))
            landings += [base, base + 1]
    started = []

    def go(hops):
        for hop in hops:
            hop.start()
        started.extend(hops)
        return hops

    def launch(number, tiles, sites, at=None):
        if number < 2:
            for i, tile in enumerate(tiles):
                out_big[number, i] = tile
        else:
            out_small[number - 2] = tiles[0]
        return go([
            Hop(
                out_big.at[number] if number < 2 else out_small.at[number - 2],
                in_big.at[number, landing] if number < 2 else in_small.at[number - 2, landing],
                send_sem.at[number, n],
                recv_sem.at[number, landing],
                site,
                at,
            )
            for n, (site, landing) in enumerate(zip(sites, landings))
        ])

    tile_row = lax.broadcasted_iota(jnp.int32, (8, LANES), 0)
    tile_lane = lax.broadcasted_iota(jnp.int32, (8, LANES), 1)
    back_half = tile_lane >= HALF

    def arrived(number, index=0, both_out=False):
        tiles = [
            in_big[number, n, index] if number < 2 else in_small[number - 2, n]
            for n in range(len(landings))
        ]
        out = tiles[slot_of[0][0]]
        for a in range(3):
            low, high = slot_of[a]
            if low == high:
                out = jnp.where(tile_row // 2 == a, tiles[low], out)
                continue
            odd = tile_row % 2 == 1
            from_up = odd if both_out else odd != back_half
            out = jnp.where(tile_row // 2 == a, jnp.where(from_up, tiles[high], tiles[low]), out)
        return out

    def wait(hops):
        for hop in hops:
            hop.wait_recv()

    for load in loads:
        load.wait()
    listed[...] = jnp.zeros_like(listed)
    listed[0:6, 0:width] = send_ref[...]
    listed[0:6, HALF : HALF + width] = send_ref[...]
    sending = listed[...]
    at_listed = Pick(sending >> 7, sending, rows)

    fields = [to_rows(ref[c : c + 1, :]) for ref in (old_ref, new_ref) for c in range(3)]
    fields = fields + [mass_ref[...]]
    for i, field in enumerate(fields + [rest_ref[...]]):
        own_fields[i] = field
    own_mass = fields[6]
    picked = [at_listed(f) for f in fields]
    picked.append(picked[6])
    tiles = [jnp.where(back_half, picked[2 * i + 1], picked[2 * i]) for i in range(BIG)]

    first = to_rows(pairs_ref[0:1, :])
    second = to_rows(pairs_ref[1:2, :])
    live = live_ref[...]
    own = second < slots
    offset = jnp.maximum(second - slots, 0)
    block = jnp.zeros_like(offset)
    for i in range(1, 6):
        block = block + jnp.where(offset >= width * i, 1, 0)
    second_row = jnp.where(own, second >> 7, rows + block)
    second_lane = jnp.where(own, second & (LANES - 1), offset - width * block)
    at_first = Pick(first >> 7, first, rows)
    at_second = Pick(second_row, second_lane, rows)
    number = (
        lax.broadcasted_iota(jnp.int32, (rows, LANES), 0) * LANES
        + lax.broadcasted_iota(jnp.int32, (rows, LANES), 1)
        + 1
    )
    counted = (live != 0) & (first != second)

    def code_row(mask_first, mask_second):
        return jnp.concatenate(
            [to_row(jnp.where(mask_first, first >> 7, -1)), to_row(jnp.where(mask_second, second_row, -1))], 1
        )

    hot = one_hot_lanes(jnp.concatenate([pairs_ref[0:1, :] & (LANES - 1), to_row(second_lane)], 1))
    number_row = to_row(number)
    number_row = jnp.concatenate([number_row, number_row + slots], 1)
    parts = [number_row >> 6, number_row & 63]
    high, low = place(code_row(counted, counted), parts, hot, rows + 8)
    ends = high * 64 + low
    ends_own = ends[:rows]
    ends_halo = ends[rows:]

    listed_row = jnp.concatenate([sending[b : b + 1, :] for b in range(6)], axis=1)
    spot = lax.broadcasted_iota(jnp.int32, listed_row.shape, 1)
    spot_lane = spot % LANES
    place_block, place_lane = place(
        jnp.where(spot_lane < width, listed_row >> 7, -1),
        [spot // LANES + 1, spot_lane],
        one_hot_lanes(listed_row & (LANES - 1)),
        rows,
    )

    minus_bit = (rows + 8) * LANES

    def coded(code):
        minus = code > slots
        index = jnp.where(minus, code - slots, code) - 1
        return jnp.where(code > 0, index + jnp.where(minus, minus_bit, 0), -1)

    def opened(code, count):
        minus = code >= minus_bit
        index = jnp.where(minus, code - minus_bit, code)
        return Pick(index >> 7, index, count), jnp.where(minus, -1.0, 1.0)

    other_first = jnp.where(counted, at_first(ends_own) - number, 0)
    other_second = jnp.where(counted & own, at_second(ends_own) - (number + slots), 0)
    far_code = jnp.where(place_block > 0, (place_block - 1) * LANES + HALF + place_lane, -1)
    reach = far_code + rows * LANES + 1
    reach = jnp.where(far_code >= 0, reach, 0)

    def partner(other, far):
        return jnp.where(other > 0, coded(other), far)

    second_code = second_row * LANES + second_lane
    lead_first = counted & ((other_first <= 0) | (number < other_first))
    lead_second = counted & own & ((other_second <= 0) | (number + slots < other_second))
    high, low = place(code_row(lead_first, lead_second), parts, hot, rows)
    lead = high * 64 + low
    send_code = jnp.where(back_half, pltpu.roll(ends_halo, HALF, 1), at_listed(ends_own))
    send_code = jnp.where(send_code > 2 * slots, 0, send_code)
    found = [
        live,
        first,
        second_code,
        partner(other_first, at_first(reach) - 1),
        partner(other_second, jnp.where(own, at_second(reach) - 1, second_code)),
        coded(send_code),
        coded(lead),
        coded(ends_own - lead),
        far_code,
    ]
    for i, code in enumerate(found):
        own_codes[i, 0 : code.shape[0]] = code

    pl.semaphore_wait(barrier, len(greeted))
    copies = launch(0, tiles, sites_home_near, here)

    def carry(index, source, end, site):
        return go([Hop(source, end, carry_sem.at[0, index], carry_sem.at[1, index], site, here)])

    inward = carry(0, own_codes, codes, greeted[0]) + carry(1, own_fields, fields_in, greeted[0])
    wait(inward)

    live, first, second_code = [codes[i, 0:rows] for i in range(3)]
    at_first = Pick(first >> 7, first, rows)
    at_second = Pick(second_code >> 7, second_code, rows + 6)
    along_first, sign_first = opened(codes[3, 0:rows], rows + 6)
    along_second, sign_second = opened(codes[4, 0:rows], rows + 6)
    to_send, send_sign = opened(codes[5, 0:8], rows)
    fields = [fields_in[i] for i in range(7)]
    mass, rest = fields[6], fields_in[7]
    near_first = [at_first(f) for f in fields]
    near_second = [at_second(f) for f in fields]

    wait(copies)
    got = [arrived(0, i, both_out=True) for i in range(BIG)]
    got_back = [pltpu.roll(t, HALF, 1) for t in got[:3]]
    halo = [got[0], got_back[0], got[1], got_back[1], got[2], got_back[2], got[3]]
    near_second = [at_second(h, rows, g, 6) for h, g in zip(halo, near_second)]
    mass_first, mass_second = near_first[6], near_second[6]
    old_span = [near_first[c] - near_second[c] for c in range(3)]
    new_span = [near_first[3 + c] - near_second[3 + c] for c in range(3)]
    dot = lambda p, q: p[0] * q[0] + p[1] * q[1] + p[2] * q[2]
    norm = jnp.sqrt(dot(old_span, old_span) + 0.25)
    unit = [s / norm for s in old_span]
    mass_sum = mass_first + mass_second
    scaling = live.astype(jnp.float32) / jnp.sqrt(mass_sum)
    weight = [scaling * u for u in unit]
    x = scaling * (dot(unit, new_span) - rest)

    copies = launch(1, [send_sign * to_send(w) for w in weight] + [to_send(x)], sites_near)
    at_lead, lead_sign = opened(codes[6, 0:rows], rows)
    at_rest, rest_sign = opened(codes[7, 0:rows], rows)
    at_far, unused = opened(codes[8, 0:rows], 6)
    diagonal = 1.0 - dot(weight, weight) * mass_sum
    pair_first = [along_first(w) for w in weight]
    pair_second = [along_second(w) for w in weight]
    lead_weight = [lead_sign * at_lead(w) for w in weight]
    rest_weight = [rest_sign * at_rest(w) for w in weight]
    near = along_first(x), along_second(x)
    wait(copies)
    got = [arrived(1, i) for i in range(BIG)]
    pair_first = [sign_first * along_first(h, rows, p, 6) for h, p in zip(got[:3], pair_first)]
    pair_second = [sign_second * along_second(h, rows, p, 6) for h, p in zip(got[:3], pair_second)]
    factor_first = -mass_first * dot(weight, pair_first)
    factor_second = mass_second * dot(weight, pair_second)
    halo_x = got[3]
    far_weight = None

    def finish(near, halo_x):
        return along_first(halo_x, rows, near[0], 6), along_second(halo_x, rows, near[1], 6)

    g = finish(near, halo_x)
    total_x, total_halo, total_g = x, halo_x, list(g)
    for index in range(2, ROUNDS):
        if index == 2 + ORDER:
            move_g = mass_first * total_g[0], mass_second * total_g[1]
            move_x = mass_sum * total_x
            stretch = [
                new_span[c] - move_x * weight[c] - move_g[0] * pair_first[c] + move_g[1] * pair_second[c]
                for c in range(3)
            ]
            length_sq = dot(stretch, stretch)
            target = jnp.sqrt(jnp.maximum(2.0 * rest * rest - length_sq, 0.25 * rest * rest))
            x = scaling * (rest - target)
        else:
            x = diagonal * x + factor_first * g[0] + factor_second * g[1]
        tile = [to_send(x)]
        if index == ROUNDS - 1:
            copies = launch(index, tile, homes_near, here)
            total_x = total_x + x
            break
        copies = launch(index, tile, sites_near)
        total_x = total_x + x
        near = along_first(x), along_second(x)
        if far_weight is None:
            far_weight = [-mass * at_far(h, stop=6) for h in got[:3]]
            for c in range(3):
                own_far[c] = far_weight[c]
            far_copy = carry(2, own_far, far_in, domain)
        wait(copies)
        halo_x = arrived(index)
        g = finish(near, halo_x)
        total_g = [t + h for t, h in zip(total_g, g)]
        total_halo = total_halo + halo_x

    at_ends = at_lead(total_x), at_rest(total_x), at_far(total_halo, stop=6)
    for c in range(3):
        own_last[c] = far_weight[c] * at_ends[2] - mass * (
            lead_weight[c] * at_ends[0] + rest_weight[c] * at_ends[1]
        )
    own_last[3] = total_x
    last_copy = carry(3, own_last, last_in, domain)
    at_far, unused = opened(far_code, 6)
    wait(far_copy)
    far_weight = [far_in[c] for c in range(3)]
    wait(copies)
    last = at_far(arrived(ROUNDS - 1), stop=6)
    wait(last_copy)
    mult_ref[...] = last_in[3]
    for c in range(3):
        move_ref[c : c + 1, :] = to_row(last_in[c] + far_weight[c] * last)
    for hop in started:
        hop.wait_send()


def solution(mesh):
    sizes = tuple(mesh.shape[a] for a in AXES)
    plan = best_plan(sizes)

    def per_device(old_pos, new_pos, inv_mass, rest_length, bond_pairs, live, send_index):
        atoms = old_pos.shape[1]
        rows = atoms // LANES
        width = send_index.shape[1]
        links = sum(1 if n == 2 else 2 for n in sizes)
        tall = lambda v: v.reshape(rows, LANES)
        vmem = pl.BlockSpec(memory_space=pltpu.VMEM)
        tile = (8, LANES)
        moved, mult = pl.pallas_call(
            functools.partial(kernel, plan, width),
            out_shape=(
                jax.ShapeDtypeStruct((3, atoms), jnp.float32),
                jax.ShapeDtypeStruct((rows, LANES), jnp.float32),
            ),
            in_specs=[pl.BlockSpec(memory_space=pl.ANY)] * 7,
            out_specs=(vmem, vmem),
            scratch_shapes=[
                pltpu.VMEM((3, atoms), jnp.float32),
                pltpu.VMEM((3, atoms), jnp.float32),
                pltpu.VMEM((rows, LANES), jnp.float32),
                pltpu.VMEM((rows, LANES), jnp.float32),
                pltpu.VMEM((2, atoms), jnp.int32),
                pltpu.VMEM((rows, LANES), jnp.int32),
                pltpu.VMEM(send_index.shape, jnp.int32),
                pltpu.VMEM(tile, jnp.int32),
                pltpu.VMEM((9, max(rows, 8), LANES), jnp.int32),
                pltpu.VMEM((9, max(rows, 8), LANES), jnp.int32),
                pltpu.VMEM((8, rows, LANES), jnp.float32),
                pltpu.VMEM((8, rows, LANES), jnp.float32),
                pltpu.VMEM((3, rows, LANES), jnp.float32),
                pltpu.VMEM((3, rows, LANES), jnp.float32),
                pltpu.VMEM((4, rows, LANES), jnp.float32),
                pltpu.VMEM((4, rows, LANES), jnp.float32),
                pltpu.VMEM((2, BIG) + tile, jnp.float32),
                pltpu.VMEM((2, links, BIG) + tile, jnp.float32),
                pltpu.VMEM((ROUNDS - 2,) + tile, jnp.float32),
                pltpu.VMEM((ROUNDS - 2, links) + tile, jnp.float32),
                pltpu.SemaphoreType.DMA((ROUNDS, links)),
                pltpu.SemaphoreType.DMA((ROUNDS, links)),
                pltpu.SemaphoreType.DMA((2, 4)),
                pltpu.SemaphoreType.DMA((7,)),
            ],
            compiler_params=pltpu.CompilerParams(collective_id=0, has_side_effects=True),
        )(old_pos, new_pos, tall(inv_mass), tall(rest_length), bond_pairs, tall(live), send_index)
        return moved, mult.reshape(atoms)

    spread = P(AXES)
    wide = P(None, AXES)
    return jax.shard_map(
        per_device,
        mesh=mesh,
        in_specs=(wide, wide, spread, spread, wide, spread, P(AXES, None)),
        out_specs=(wide, spread),
        check_vma=False,
    )
```

time: 47.1 us -> 40.5 us (0.86)
  Pallas kernels: 44.3 us -> 37.7 us
    pallas_call x1, Pallas kernels: 44.3 us -> 37.7 us  [per_device(): pl.pallas_call(functools.partial(kernel, plan, width), out_shape=(jax.Sha...]
where the time goes in v2:
time: 40.5 us; the launch traced here: 40.3 us
  Pallas kernels  37.7 us (93%)
  local copies, waits for them, and re-layouts  1.92 us (5%)
  between operations  0.65 us (2%)
    pallas_call x1, Pallas kernels, per_device(): pl.pallas_call(functools.partial(kernel, plan, width), out_shape=(jax.Sha...  37.7 us
    unnamed x4, local copies, waits for them, and re-layouts  1.92 us

profile of v2, /device:TPU:0, one launch (start us, length us, event | category | flops | bytes accessed | tf_op | source)
XLA Modules:
  0.0 40.3 jit_solution(4017585861398214111)
XLA Ops:
  0.6 37.7 %shard_map.86 = (f32[3,1024]{1,0:T(4,128)}, f32[8,128]{1,0:T(8,128)}) custom-call(f32[3,1024]{1,0:T(4,128)} %refs_0_.1, f32[3,1024]{1,0:T(4,128)} %refs_1_.1, f32[8,128]{1,0:T(8,128)} %bitcast.4, f32[8,128]{1,0:T(8,128)} %bitcast.5, s32[2,1024]{1,0:T(2,128)} %refs_4_.1, s32[8,128]{1,0:T(8,128)} %bitcast.6, s32[6,48]{1,0:T(8,128)} %refs_6_.1), custom_call_target="tpu_custom_call" | custom-call | tf_op jit(solution)/shard_map/pallas_call | solution.py:460
  38.3 0.0 copy-start
  38.4 1.3 %copy.11 = f32[3,1024]{1,0:T(4,128)} copy(f32[3,1024]{1,0:T(4,128)} %get-tuple-element.8) | data formatting | bytes 24576
  39.7 0.0 copy-done
  39.7 0.6 %copy.12 = f32[1024]{0:T(1024)} copy(f32[1024]{0:T(1024)S(1)} %bitcast.7) | data formatting | bytes 8192
Async XLA Ops:
  38.3 1.3 %copy-start = (f32[8,128]{1,0:T(8,128)S(1)}, f32[8,128]{1,0:T(8,128)}, u32[]{:S(2)}) copy-start(f32[8,128]{1,0:T(8,128)} %get-tuple-element.5) | copy-start | bytes 12292

commit v3 on v2

--- a/solution.py
+++ b/solution.py
@@ -334,12 +334,13 @@
         own_codes[i, 0 : code.shape[0]] = code
 
     pl.semaphore_wait(barrier, len(greeted))
-    copies = launch(0, tiles, sites_home_near, here)
-
     def carry(index, source, end, site):
         return go([Hop(source, end, carry_sem.at[0, index], carry_sem.at[1, index], site, here)])
 
-    inward = carry(0, own_codes, codes, greeted[0]) + carry(1, own_fields, fields_in, greeted[0])
+    inward = carry(0, own_codes.at[0:6], codes.at[0:6], greeted[0])
+    inward += carry(1, own_fields, fields_in, greeted[0])
+    copies = launch(0, tiles, sites_home_near, here)
+    later = carry(4, own_codes.at[6:9], codes.at[6:9], greeted[0])
     wait(inward)
 
     live, first, second_code = [codes[i, 0:rows] for i in range(3)]
@@ -370,6 +371,7 @@
     x = scaling * (dot(unit, new_span) - rest)
 
     copies = launch(1, [send_sign * to_send(w) for w in weight] + [to_send(x)], sites_near)
+    wait(later)
     at_lead, lead_sign = opened(codes[6, 0:rows], rows)
     at_rest, rest_sign = opened(codes[7, 0:rows], rows)
     at_far, unused = opened(codes[8, 0:rows], 6)
@@ -460,8 +462,8 @@
         moved, mult = pl.pallas_call(
             functools.partial(kernel, plan, width),
             out_shape=(
-                jax.ShapeDtypeStruct((3, atoms), jnp.float32),
-                jax.ShapeDtypeStruct((rows, LANES), jnp.float32),
+                pltpu.VMEM((3, atoms), jnp.float32),
+                pltpu.VMEM((rows, LANES), jnp.float32),
             ),
             in_specs=[pl.BlockSpec(memory_space=pl.ANY)] * 7,
             out_specs=(vmem, vmem),
@@ -488,7 +490,7 @@
                 pltpu.VMEM((ROUNDS - 2, links) + tile, jnp.float32),
                 pltpu.SemaphoreType.DMA((ROUNDS, links)),
                 pltpu.SemaphoreType.DMA((ROUNDS, links)),
-                pltpu.SemaphoreType.DMA((2, 4)),
+                pltpu.SemaphoreType.DMA((2, 5)),
                 pltpu.SemaphoreType.DMA((7,)),
             ],
             compiler_params=pltpu.CompilerParams(collective_id=0, has_side_effects=True),

time: 40.5 us -> 38.7 us (0.956)
  Pallas kernels: 37.7 us -> 36.6 us
  local copies, waits for them, and re-layouts: 1.92 us -> 1.2 us
    pallas_call x1, Pallas kernels: 37.7 us -> 36.6 us  [per_device(): pl.pallas_call(functools.partial(kernel, plan, width), out_shape=(pltpu.V...]
    unnamed x4 -> x2, local copies, waits for them, and re-layouts: 1.92 us -> 1.2 us
where the time goes in v3:
time: 38.7 us; the launch traced here: 38.4 us
  Pallas kernels  36.6 us (95%)
  local copies, waits for them, and re-layouts  1.2 us (3%)
  between operations  0.64 us (2%)
    pallas_call x1, Pallas kernels, per_device(): pl.pallas_call(functools.partial(kernel, plan, width), out_shape=(pltpu.V...  36.6 us
    unnamed x2, local copies, waits for them, and re-layouts  1.2 us

profile of v3, /device:TPU:0, one launch (start us, length us, event | category | flops | bytes accessed | tf_op | source)
XLA Modules:
  0.0 38.4 jit_solution(7499252377899525776)
XLA Ops:
  0.6 36.6 %shard_map.86 = (f32[3,1024]{1,0:T(4,128)S(1)}, f32[8,128]{1,0:T(8,128)S(1)}) custom-call(f32[3,1024]{1,0:T(4,128)} %refs_0_.1, f32[3,1024]{1,0:T(4,128)} %refs_1_.1, f32[8,128]{1,0:T(8,128)} %bitcast.5, f32[8,128]{1,0:T(8,128)} %bitcast.6, s32[2,1024]{1,0:T(2,128)} %refs_4_.1, s32[8,128]{1,0:T(8,128)} %bitcast.7, s32[6,48]{1,0:T(8,128)} %refs_6_.1), custom_call_target="tpu_custom_call" | custom-call | tf_op jit(solution)/shard_map/pallas_call | solution.py:462
  37.2 0.6 %copy.11 = f32[3,1024]{1,0:T(4,128)} copy(f32[3,1024]{1,0:T(4,128)S(1)} %get-tuple-element.6) | data formatting | bytes 24576
  37.8 0.6 %copy.12 = f32[1024]{0:T(1024)} copy(f32[1024]{0:T(1024)S(1)} %bitcast.4) | data formatting | bytes 8192

commit v4 on v3

--- a/solution.py
+++ b/solution.py
@@ -109,10 +109,12 @@
         self.masks = [row == r for r in range(count)]
 
     def __call__(self, table, start=0, init=None, stop=None):
-        out = jnp.zeros(self.lane.shape, table.dtype) if init is None else init
-        count = table.shape[0] if stop is None else stop
-        for r in range(count):
-            line = jnp.broadcast_to(table[r : r + 1, :], self.lane.shape)
+        if not isinstance(table, list):
+            count = table.shape[0] if stop is None else stop
+            table = [table[r : r + 1, :] for r in range(count)]
+        out = jnp.zeros(self.lane.shape, table[0].dtype) if init is None else init
+        for r, line in enumerate(table):
+            line = jnp.broadcast_to(line, self.lane.shape)
             found = jnp.take_along_axis(line, self.lane, axis=1, mode="promise_in_bounds")
             out = jnp.where(self.masks[start + r], found, out)
         return out
@@ -172,15 +174,17 @@
     for load in loads:
         load.start()
 
-    slot_of, landings = [], []
-    for n in sizes:
+    slot_of, landings, axis_of = [], [], []
+    for a, n in enumerate(sizes):
         base = len(landings)
         if n == 2:
             slot_of.append((base, base))
             landings.append(base)
+            axis_of.append(a)
         else:
             slot_of.append((base, base + 1))
             landings += [base, base + 1]
+            axis_of += [a, a]
     started = []
 
     def go(hops):
@@ -191,13 +195,13 @@
 
     def launch(number, tiles, sites, at=None):
         if number < 2:
-            for i, tile in enumerate(tiles):
-                out_big[number, i] = tile
+            for a in range(3):
+                out_big[number, a] = jnp.concatenate([t[2 * a : 2 * a + 2] for t in tiles], axis=0)
         else:
             out_small[number - 2] = tiles[0]
         return go([
             Hop(
-                out_big.at[number] if number < 2 else out_small.at[number - 2],
+                out_big.at[number, axis_of[n]] if number < 2 else out_small.at[number - 2],
                 in_big.at[number, landing] if number < 2 else in_small.at[number - 2, landing],
                 send_sem.at[number, n],
                 recv_sem.at[number, landing],
@@ -211,20 +215,17 @@
     tile_lane = lax.broadcasted_iota(jnp.int32, (8, LANES), 1)
     back_half = tile_lane >= HALF
 
-    def arrived(number, index=0, both_out=False):
-        tiles = [
-            in_big[number, n, index] if number < 2 else in_small[number - 2, n]
-            for n in range(len(landings))
-        ]
-        out = tiles[slot_of[0][0]]
-        for a in range(3):
-            low, high = slot_of[a]
-            if low == high:
-                out = jnp.where(tile_row // 2 == a, tiles[low], out)
-                continue
-            odd = tile_row % 2 == 1
-            from_up = odd if both_out else odd != back_half
-            out = jnp.where(tile_row // 2 == a, jnp.where(from_up, tiles[high], tiles[low]), out)
+    def merged(tiles, a):
+        low, high = slot_of[a]
+        if low == high:
+            return tiles[low]
+        return jnp.where((tile_row % 2 == 1) != back_half, tiles[high], tiles[low])
+
+    def arrived(number):
+        tiles = [in_small[number - 2, n] for n in range(len(landings))]
+        out = merged(tiles, 0)
+        for a in range(1, 3):
+            out = jnp.where(tile_row // 2 == a, merged(tiles, a), out)
         return out
 
     def wait(hops):
@@ -355,9 +356,16 @@
     near_second = [at_second(f) for f in fields]
 
     wait(copies)
-    got = [arrived(0, i, both_out=True) for i in range(BIG)]
-    got_back = [pltpu.roll(t, HALF, 1) for t in got[:3]]
-    halo = [got[0], got_back[0], got[1], got_back[1], got[2], got_back[2], got[3]]
+    tiles = [in_big[0, n] for n in range(len(landings))]
+    turned = [pltpu.roll(t, HALF, 1) for t in tiles]
+    halo = []
+    for i in range(7):
+        source, t = (turned if i % 2 else tiles), i // 2
+        halo.append([
+            source[slot_of[a][side]][2 * t + side : 2 * t + side + 1]
+            for a in range(3)
+            for side in range(2)
+        ])
     near_second = [at_second(h, rows, g, 6) for h, g in zip(halo, near_second)]
     mass_first, mass_second = near_first[6], near_second[6]
     old_span = [near_first[c] - near_second[c] for c in range(3)]
@@ -382,12 +390,19 @@
     rest_weight = [rest_sign * at_rest(w) for w in weight]
     near = along_first(x), along_second(x)
     wait(copies)
-    got = [arrived(1, i) for i in range(BIG)]
+    tiles = [in_big[1, n] for n in range(len(landings))]
+    tiles = [merged(tiles, a) for a in range(3)]
+    got = [
+        [tiles[a][2 * t + side : 2 * t + side + 1] for a in range(3) for side in range(2)]
+        for t in range(BIG - 1)
+    ]
+    halo_x = jnp.concatenate(
+        [t[2 * BIG - 2 : 2 * BIG] for t in tiles] + [jnp.zeros((2, LANES), jnp.float32)], axis=0
+    )
     pair_first = [sign_first * along_first(h, rows, p, 6) for h, p in zip(got[:3], pair_first)]
     pair_second = [sign_second * along_second(h, rows, p, 6) for h, p in zip(got[:3], pair_second)]
     factor_first = -mass_first * dot(weight, pair_first)
     factor_second = mass_second * dot(weight, pair_second)
-    halo_x = got[3]
     far_weight = None
 
     def finish(near, halo_x):
@@ -484,8 +499,8 @@
                 pltpu.VMEM((3, rows, LANES), jnp.float32),
                 pltpu.VMEM((4, rows, LANES), jnp.float32),
                 pltpu.VMEM((4, rows, LANES), jnp.float32),
-                pltpu.VMEM((2, BIG) + tile, jnp.float32),
-                pltpu.VMEM((2, links, BIG) + tile, jnp.float32),
+                pltpu.VMEM((2, 3) + tile, jnp.float32),
+                pltpu.VMEM((2, links) + tile, jnp.float32),
                 pltpu.VMEM((ROUNDS - 2,) + tile, jnp.float32),
                 pltpu.VMEM((ROUNDS - 2, links) + tile, jnp.float32),
                 pltpu.SemaphoreType.DMA((ROUNDS, links)),

time: 38.7 us -> 37.9 us (0.979)
  Pallas kernels: 36.6 us -> 35.8 us
    pallas_call x1, Pallas kernels: 36.6 us -> 35.8 us  [per_device(): pl.pallas_call(functools.partial(kernel, plan, width), out_shape=(pltpu.V...]
where the time goes in v4:
time: 37.9 us; the launch traced here: 37.6 us
  Pallas kernels  35.8 us (94%)
  local copies, waits for them, and re-layouts  1.2 us (3%)
  between operations  0.64 us (2%)
    pallas_call x1, Pallas kernels, per_device(): pl.pallas_call(functools.partial(kernel, plan, width), out_shape=(pltpu.V...  35.8 us
    unnamed x2, local copies, waits for them, and re-layouts  1.2 us

profile of v4, /device:TPU:0, one launch (start us, length us, event | category | flops | bytes accessed | tf_op | source)
XLA Modules:
  0.0 37.6 jit_solution(16661978322953004639)
XLA Ops:
  0.6 35.8 %shard_map.86 = (f32[3,1024]{1,0:T(4,128)S(1)}, f32[8,128]{1,0:T(8,128)S(1)}) custom-call(f32[3,1024]{1,0:T(4,128)} %refs_0_.1, f32[3,1024]{1,0:T(4,128)} %refs_1_.1, f32[8,128]{1,0:T(8,128)} %bitcast.5, f32[8,128]{1,0:T(8,128)} %bitcast.6, s32[2,1024]{1,0:T(2,128)} %refs_4_.1, s32[8,128]{1,0:T(8,128)} %bitcast.7, s32[6,48]{1,0:T(8,128)} %refs_6_.1), custom_call_target="tpu_custom_call" | custom-call | tf_op jit(solution)/shard_map/pallas_call | solution.py:477
  36.4 0.6 %copy.11 = f32[3,1024]{1,0:T(4,128)} copy(f32[3,1024]{1,0:T(4,128)S(1)} %get-tuple-element.6) | data formatting | bytes 24576
  37.0 0.6 %copy.12 = f32[1024]{0:T(1024)} copy(f32[1024]{0:T(1024)S(1)} %bitcast.4) | data formatting | bytes 8192

commit v5 on v4

--- a/solution.py
+++ b/solution.py
@@ -198,10 +198,11 @@
             for a in range(3):
                 out_big[number, a] = jnp.concatenate([t[2 * a : 2 * a + 2] for t in tiles], axis=0)
         else:
-            out_small[number - 2] = tiles[0]
+            for a in range(3):
+                out_small[number - 2, a] = tiles[0][2 * a : 2 * a + 2]
         return go([
             Hop(
-                out_big.at[number, axis_of[n]] if number < 2 else out_small.at[number - 2],
+                out_big.at[number, axis_of[n]] if number < 2 else out_small.at[number - 2, axis_of[n]],
                 in_big.at[number, landing] if number < 2 else in_small.at[number - 2, landing],
                 send_sem.at[number, n],
                 recv_sem.at[number, landing],
@@ -215,18 +216,20 @@
     tile_lane = lax.broadcasted_iota(jnp.int32, (8, LANES), 1)
     back_half = tile_lane >= HALF
 
+    upper = (tile_row % 2 == 1) != back_half
+
     def merged(tiles, a):
         low, high = slot_of[a]
         if low == high:
             return tiles[low]
-        return jnp.where((tile_row % 2 == 1) != back_half, tiles[high], tiles[low])
+        return jnp.where(upper[: tiles[low].shape[0]], tiles[high], tiles[low])
 
     def arrived(number):
         tiles = [in_small[number - 2, n] for n in range(len(landings))]
-        out = merged(tiles, 0)
-        for a in range(1, 3):
-            out = jnp.where(tile_row // 2 == a, merged(tiles, a), out)
-        return out
+        return [merged(tiles, a) for a in range(3)]
+
+    def lines(pairs):
+        return [pair[side : side + 1] for pair in pairs for side in range(2)]
 
     def wait(hops):
         for hop in hops:
@@ -396,9 +399,7 @@
         [tiles[a][2 * t + side : 2 * t + side + 1] for a in range(3) for side in range(2)]
         for t in range(BIG - 1)
     ]
-    halo_x = jnp.concatenate(
-        [t[2 * BIG - 2 : 2 * BIG] for t in tiles] + [jnp.zeros((2, LANES), jnp.float32)], axis=0
-    )
+    halo_x = [t[2 * BIG - 2 : 2 * BIG] for t in tiles]
     pair_first = [sign_first * along_first(h, rows, p, 6) for h, p in zip(got[:3], pair_first)]
     pair_second = [sign_second * along_second(h, rows, p, 6) for h, p in zip(got[:3], pair_second)]
     factor_first = -mass_first * dot(weight, pair_first)
@@ -406,7 +407,8 @@
     far_weight = None
 
     def finish(near, halo_x):
-        return along_first(halo_x, rows, near[0], 6), along_second(halo_x, rows, near[1], 6)
+        halo_x = lines(halo_x)
+        return along_first(halo_x, rows, near[0]), along_second(halo_x, rows, near[1])
 
     g = finish(near, halo_x)
     total_x, total_halo, total_g = x, halo_x, list(g)
@@ -440,9 +442,9 @@
         halo_x = arrived(index)
         g = finish(near, halo_x)
         total_g = [t + h for t, h in zip(total_g, g)]
-        total_halo = total_halo + halo_x
-
-    at_ends = at_lead(total_x), at_rest(total_x), at_far(total_halo, stop=6)
+        total_halo = [t + h for t, h in zip(total_halo, halo_x)]
+
+    at_ends = at_lead(total_x), at_rest(total_x), at_far(lines(total_halo))
     for c in range(3):
         own_last[c] = far_weight[c] * at_ends[2] - mass * (
             lead_weight[c] * at_ends[0] + rest_weight[c] * at_ends[1]
@@ -453,7 +455,7 @@
     wait(far_copy)
     far_weight = [far_in[c] for c in range(3)]
     wait(copies)
-    last = at_far(arrived(ROUNDS - 1), stop=6)
+    last = at_far(lines(arrived(ROUNDS - 1)))
     wait(last_copy)
     mult_ref[...] = last_in[3]
     for c in range(3):
@@ -501,8 +503,8 @@
                 pltpu.VMEM((4, rows, LANES), jnp.float32),
                 pltpu.VMEM((2, 3) + tile, jnp.float32),
                 pltpu.VMEM((2, links) + tile, jnp.float32),
-                pltpu.VMEM((ROUNDS - 2,) + tile, jnp.float32),
-                pltpu.VMEM((ROUNDS - 2, links) + tile, jnp.float32),
+                pltpu.VMEM((ROUNDS - 2, 3, 2, LANES), jnp.float32),
+                pltpu.VMEM((ROUNDS - 2, links, 2, LANES), jnp.float32),
                 pltpu.SemaphoreType.DMA((ROUNDS, links)),
                 pltpu.SemaphoreType.DMA((ROUNDS, links)),
                 pltpu.SemaphoreType.DMA((2, 5)),

time: 37.9 us -> 37.5 us (0.989)
  Pallas kernels: 35.8 us -> 35.4 us
where the time goes in v5:
time: 37.5 us; the launch traced here: 37.3 us
  Pallas kernels  35.4 us (94%)
  local copies, waits for them, and re-layouts  1.2 us (3%)
  between operations  0.64 us (2%)
    pallas_call x1, Pallas kernels, per_device(): pl.pallas_call(functools.partial(kernel, plan, width), out_shape=(pltpu.V...  35.4 us
    unnamed x2, local copies, waits for them, and re-layouts  1.2 us

profile of v5, /device:TPU:0, one launch (start us, length us, event | category | flops | bytes accessed | tf_op | source)
XLA Modules:
  0.0 37.3 jit_solution(7481101749033487331)
XLA Ops:
  0.6 35.4 %shard_map.86 = (f32[3,1024]{1,0:T(4,128)S(1)}, f32[8,128]{1,0:T(8,128)S(1)}) custom-call(f32[3,1024]{1,0:T(4,128)} %refs_0_.1, f32[3,1024]{1,0:T(4,128)} %refs_1_.1, f32[8,128]{1,0:T(8,128)} %bitcast.5, f32[8,128]{1,0:T(8,128)} %bitcast.6, s32[2,1024]{1,0:T(2,128)} %refs_4_.1, s32[8,128]{1,0:T(8,128)} %bitcast.7, s32[6,48]{1,0:T(8,128)} %refs_6_.1), custom_call_target="tpu_custom_call" | custom-call | tf_op jit(solution)/shard_map/pallas_call | solution.py:479
  36.1 0.6 %copy.11 = f32[3,1024]{1,0:T(4,128)} copy(f32[3,1024]{1,0:T(4,128)S(1)} %get-tuple-element.6) | data formatting | bytes 24576
  36.7 0.6 %copy.12 = f32[1024]{0:T(1024)} copy(f32[1024]{0:T(1024)S(1)} %bitcast.4) | data formatting | bytes 8192
